TPU v7x, 32 devices: a whole 2x2x4 slice. The times are simulated.
32 devices in a mesh: groups: 2 (over y), section: 2 (over x), expert: 4 (over z), pair: 2 (over core).
Axes of the slice: x: 2, y: 2, z: 4, core: 2. Of those that a mesh axis runs over, the one named last changes fastest.
Arguments:
- transit_activation: bfloat16 [2, 32, 3072], P('section', ('groups', 'expert', 'pair')), parts along dimension 1, may hold values from -6 to 6
- incoming_queue: bfloat16 [2, 32, 3072], P('section', ('groups', 'expert', 'pair')), parts along dimension 1, may hold values from -6 to 6
- expert_assignment: int32 [2, 3, 32, 1], P('section', None, ('groups', 'expert', 'pair')), parts along dimension 2, may hold values from 0 to 1; in each aligned block of 2 rows (0 to 1, 2 to 3, ..., all dimensions but the last counted through in order) at most 2 rows name the same one
- rescale_factor: float32 [2, 3072], P('section'), may hold values from 0.25 to 1.75
- routing_matrix: bfloat16 [2, 3072, 2], P('section'), may hold values from -0.109375 to 0.109375
- gating_matrix: bfloat16 [2, 2, 3072, 8192], P('section', 'pair', None, 'expert'), may hold values from -0.109375 to 0.109375
- expand_matrix: bfloat16 [2, 2, 3072, 8192], P('section', 'pair', None, 'expert'), may hold values from -0.109375 to 0.109375
- contract_matrix: bfloat16 [2, 2, 8192, 3072], P('section', 'pair', 'expert'), may hold values from -0.0625 to 0.0625
Outputs:
- inflight_out: bfloat16 [2, 32, 3072], P('section', ('groups', 'expert', 'pair')), parts along dimension 1
- finished: bfloat16 [2, 32, 3072], P('section', ('groups', 'expert', 'pair')), parts along dimension 1
There are 2 independent parts, one for each index of `groups`. A program takes and returns all parts, laid end to end along the dimension named above; an argument that names none is the same for every part. Nothing has to cross between parts.
Inputs may be any that keep to these rules, and one draw needn't show every extreme that they name: `expert_assignment`: the expert chosen by each token of each layer and tick. In each aligned block of 2 rows, no expert is chosen by more than 2 rows.
All inputs are finite; a program needn't handle non-finite values.
Results may differ from a plain program's by a relative error of at most 0.023.
Values may be sent and summed in bfloat16 or wider, within the bound.
A program may use at most 64 MiB of HBM per device.

v0:
```python
import jax
import jax.numpy as jnp
from jax import lax
from jax.sharding import PartitionSpec as P

EPSILON = 1e-06


def shifted(block, axis, distance):
    devices = range(lax.axis_size(axis))
    route = [((i - distance) % len(devices), i) for i in devices]
    return lax.ppermute(block, axis, route)


def expand(rows, gate_w, up_w):
    gate = jnp.dot(rows, gate_w, preferred_element_type=jnp.float32)
    upper = jnp.dot(rows, up_w, preferred_element_type=jnp.float32)
    return (jax.nn.silu(gate) * upper).astype(jnp.bfloat16)


def moe_layer(rows, picks, gain, table, gate_w, up_w, down_w):
    tokens_here, width = rows.shape
    experts = table.shape[1]
    wide = rows.astype(jnp.float32)
    square = jnp.mean(wide * wide, axis=-1, keepdims=True)
    normed = (wide * lax.rsqrt(square + EPSILON) * gain).astype(jnp.bfloat16)
    logits = jnp.dot(normed, table, preferred_element_type=jnp.float32)
    pick = picks[:, 0]
    chosen = jnp.where(pick == 0, logits[:, 0], logits[:, 1])
    other = jnp.where(pick == 0, logits[:, 1], logits[:, 0])
    weight = jax.nn.sigmoid(chosen - other)[:, None]
    flags = (pick[:, None] == lax.broadcasted_iota(jnp.int32, (1, experts), 1)).astype(jnp.int32)
    before = jnp.cumsum(flags, axis=0) - flags
    slot = jnp.sum(before * flags, axis=-1)
    target = pick * tokens_here + slot
    slots_all = experts * tokens_here
    lookup = (target[:, None] == lax.broadcasted_iota(jnp.int32, (1, slots_all), 1)).astype(
        jnp.bfloat16
    )
    outgoing = jnp.dot(lookup.T, normed, preferred_element_type=jnp.float32).astype(jnp.bfloat16)
    parcel = outgoing.reshape(experts, tokens_here, width)
    arrived = lax.all_to_all(parcel, "pair", split_axis=0, concat_axis=0, tiled=True)
    hidden = expand(
        lax.all_gather(arrived.reshape(slots_all, width), "expert", axis=0, tiled=True),
        gate_w,
        up_w,
    )
    summed = lax.psum_scatter(
        jnp.dot(hidden, down_w, preferred_element_type=jnp.float32).astype(jnp.bfloat16),
        "expert",
        scatter_dimension=0,
        tiled=True,
    )
    answer = summed.reshape(experts, tokens_here, width)
    back = lax.all_to_all(answer, "pair", split_axis=0, concat_axis=0, tiled=True).reshape(
        slots_all, width
    )
    picked = jnp.dot(lookup, back, preferred_element_type=jnp.float32)
    return (wide + weight * picked).astype(jnp.bfloat16)


def body(
    transit_activation,
    incoming_queue,
    expert_assignment,
    rescale_factor,
    routing_matrix,
    gating_matrix,
    expand_matrix,
    contract_matrix,
):
    head = lax.axis_index("section") == 0
    ticks = expert_assignment.shape[1]
    gain = rescale_factor[0]
    table = routing_matrix[0]
    gate_w = gating_matrix[0, 0]
    up_w = expand_matrix[0, 0]
    down_w = contract_matrix[0, 0]
    working_level = transit_activation[0]
    waiting = incoming_queue[0]
    for tick in range(ticks):
        working_level = moe_layer(
            working_level, expert_assignment[0, tick], gain, table, gate_w, up_w, down_w
        )
        moved_now, moved_side = shifted((working_level, waiting), "section", 1)
        working_level = jnp.where(head, moved_side, moved_now)
        waiting = jnp.where(head, moved_now, moved_side)
    return (working_level[None], waiting[None])


def solution(mesh):
    in_specs = (
        P("section", ("groups", "expert", "pair"), None),
        P("section", ("groups", "expert", "pair"), None),
        P("section", None, ("groups", "expert", "pair"), None),
        P("section", None),
        P("section", None, None),
        P("section", "pair", None, "expert"),
        P("section", "pair", None, "expert"),
        P("section", "pair", "expert", None),
    )
    out_specs = (
        P("section", ("groups", "expert", "pair"), None),
        P("section", ("groups", "expert", "pair"), None),
    )
    return jax.shard_map(body, mesh=mesh, in_specs=in_specs, out_specs=out_specs, check_vma=False)
```

profile of v0, /device:TPU:0, one launch (start us, length us, event | category | flops | bytes accessed | tf_op | source)
XLA Modules:
  0.0 261.2 jit_solution(6238528714647378874)
XLA Ops:
  7.2 3.0 %collective-permute-start = (bf16[2,3072]{1,0:T(2,128)(2,1)}, bf16[2,3072]{1,0:T(2,128)(2,1)S(1)}, u32[]{:S(2)}, u32[]{:S(2)}) collective-permute-start(bf16[2,3072]{1,0:T(2,128)(2,1)} %bitcast.139), channel_id=1, source_target_pairs={{8,0},{0,8},{9,1},{1,9},{10,2},{2,10},{11,3},{3,11},{12,4},{4,12},... | collective-permute-start | bytes 36872 | tf_op jit(solution)/shard_map/ppermute | solution.py:12
  10.3 0.8 fusion.77
  11.1 1.0 slice_reduce_fusion
  12.4 1.0 convolution_convert_fusion.2
  13.5 3.7 %all_to_all.30 = bf16[2,2,3072]{2,1,0:T(2,128)(2,1)S(1)} all-to-all(bf16[2,2,3072]{2,1,0:T(2,128)(2,1)S(1)} %reshape.143), channel_id=1, replica_groups=mesh['groups'=2,'section'=2,'expert'=4,'pair'=2] {'pair'}, dimensions={0} | all-to-all | bytes 49152 | tf_op jit(solution)/shard_map/all_to_all | solution.py:42
  17.2 13.6 %all-gather = bf16[4,4,3072]{2,1,0:T(4,128)(2,1)S(1)} all-gather(bf16[1,4,3072]{2,1,0:T(4,128)(2,1)S(1)} %reshape.156), channel_id=1, replica_groups=mesh['groups'=2,'section'=2,'expert'=4,'pair'=2] {'expert'}, dimensions={0}, use_global_device_ids=true | all-gather | bytes 122880 | tf_op jit(solution)/shard_map/all_gather | solution.py:44
  30.8 6.3 %fusion.16 = f32[16,2048]{1,0:T(8,128)S(1)} fusion(bf16[16,3072]{1,0:T(8,128)(2,1)S(1)} %reshape.157, bf16[1,1,3072,2048]{3,2,1,0:T(8,128)(2,1)} %param.13), kind=kOutput, calls=%fused_computation.16 | convolution fusion | flops 201326592 | bytes 12812288 | tf_op jit(solution)/shard_map/dot_general | solution.py:16
  37.2 12.2 %fusion.18 = bf16[16,3072]{1,0:T(8,128)(2,1)} fusion(bf16[1,1,2048,3072]{3,2,1,0:T(8,128)(2,1)} %param.15, bf16[16,3072]{1,0:T(8,128)(2,1)S(1)} %reshape.157, bf16[1,1,3072,2048]{3,2,1,0:T(8,128)(2,1)} %param.14, f32[16,2048]{1,0:T(8,128)S(1)} %fusion.16), kind=kOutput, calls=%fused_computation.18 | convolution fusion | flops 402898944 | bytes 25493504 | tf_op jit(solution)/shard_map/dot_general | solution.py:49
  51.6 32.5 %all-reduce.7.cloned.1.call-done = bf16[16,3072]{1,0:T(8,128)(2,1)} async-done(((bf16[16,3072]{1,0:T(8,128)(2,1)}), bf16[16,3072]{1,0:T(8,128)(2,1)}) %all-reduce.7.cloned.1.call-update) | async-done | bytes 98320
  84.1 0.8 constant_dynamic-slice_fusion.2
  84.9 3.7 %all_to_all.31 = bf16[2,2,3072]{2,1,0:T(2,128)(2,1)S(1)} all-to-all(bf16[2,2,3072]{2,1,0:T(2,128)(2,1)S(1)} %reshape.145), channel_id=1, replica_groups=mesh['groups'=2,'section'=2,'expert'=4,'pair'=2] {'pair'}, dimensions={0} | all-to-all | bytes 49152 | tf_op jit(solution)/shard_map/all_to_all | solution.py:55
  88.9 1.5 collective-permute-start.1
  90.6 2.0 collective-permute-done.1
  93.9 3.2 %all-to-all-start.2 = ((bf16[2,2,3072]{2,1,0:T(2,128)(2,1)}), bf16[2,2,3072]{2,1,0:T(2,128)(2,1)S(1)}, u32[]{:S(2)}, u32[]{:S(2)}) async-start(bf16[2,2,3072]{2,1,0:T(2,128)(2,1)} %reshape.147), calls=%async_computation.2 | async-start | bytes 49152 | tf_op jit(solution)/shard_map/all_to_all | solution.py:42
  97.2 1.5 collective-permute-start.3
  98.8 13.4 %all-gather.1 = bf16[4,4,3072]{2,1,0:T(4,128)(2,1)S(1)} all-gather(bf16[1,4,3072]{2,1,0:T(4,128)(2,1)S(1)} %reshape.158), channel_id=1, replica_groups=mesh['groups'=2,'section'=2,'expert'=4,'pair'=2] {'expert'}, dimensions={0}, use_global_device_ids=true | all-gather | bytes 122880 | tf_op jit(solution)/shard_map/all_gather | solution.py:44
  112.2 6.3 %fusion.14 = f32[16,2048]{1,0:T(8,128)S(1)} fusion(bf16[16,3072]{1,0:T(8,128)(2,1)S(1)} %reshape.159, bf16[1,1,3072,2048]{3,2,1,0:T(8,128)(2,1)} %param.13), kind=kOutput, calls=%fused_computation.14 | convolution fusion | flops 201326592 | bytes 12812288 | tf_op jit(solution)/shard_map/dot_general | solution.py:16
  118.5 12.2 %fusion.21 = bf16[16,3072]{1,0:T(8,128)(2,1)} fusion(bf16[1,1,2048,3072]{3,2,1,0:T(8,128)(2,1)} %param.15, bf16[16,3072]{1,0:T(8,128)(2,1)S(1)} %reshape.159, bf16[1,1,3072,2048]{3,2,1,0:T(8,128)(2,1)} %param.14, f32[16,2048]{1,0:T(8,128)S(1)} %fusion.14), kind=kOutput, calls=%fused_computation.19 | convolution fusion | flops 402898944 | bytes 25493504 | tf_op jit(solution)/shard_map/dot_general | solution.py:49
  130.9 33.9 %all-reduce.9.cloned.1.call-done = bf16[16,3072]{1,0:T(8,128)(2,1)} async-done(((bf16[16,3072]{1,0:T(8,128)(2,1)}), bf16[16,3072]{1,0:T(8,128)(2,1)}) %all-reduce.9.cloned.1.call-update) | async-done | bytes 98320
  164.9 0.8 constant_dynamic-slice_fusion.1
  165.7 3.7 %all_to_all.32 = bf16[2,2,3072]{2,1,0:T(2,128)(2,1)S(1)} all-to-all(bf16[2,2,3072]{2,1,0:T(2,128)(2,1)S(1)} %reshape.149), channel_id=1, replica_groups=mesh['groups'=2,'section'=2,'expert'=4,'pair'=2] {'pair'}, dimensions={0} | all-to-all | bytes 49152 | tf_op jit(solution)/shard_map/all_to_all | solution.py:55
  169.7 1.5 collective-permute-start.2
  171.2 2.2 collective-permute-done.2
  174.7 3.2 %all-to-all-start.4 = ((bf16[2,2,3072]{2,1,0:T(2,128)(2,1)}), bf16[2,2,3072]{2,1,0:T(2,128)(2,1)S(1)}, u32[]{:S(2)}, u32[]{:S(2)}) async-start(bf16[2,2,3072]{2,1,0:T(2,128)(2,1)} %reshape.151), calls=%async_computation.4 | async-start | bytes 49152 | tf_op jit(solution)/shard_map/all_to_all | solution.py:42
  178.0 1.5 collective-permute-start.4
  179.6 13.2 %all-gather.2 = bf16[4,4,3072]{2,1,0:T(4,128)(2,1)S(1)} all-gather(bf16[1,4,3072]{2,1,0:T(4,128)(2,1)S(1)} %reshape.160), channel_id=1, replica_groups=mesh['groups'=2,'section'=2,'expert'=4,'pair'=2] {'expert'}, dimensions={0}, use_global_device_ids=true | all-gather | bytes 122880 | tf_op jit(solution)/shard_map/all_gather | solution.py:44
  192.8 6.3 %fusion.12 = f32[16,2048]{1,0:T(8,128)S(1)} fusion(bf16[16,3072]{1,0:T(8,128)(2,1)S(1)} %reshape.161, bf16[1,1,3072,2048]{3,2,1,0:T(8,128)(2,1)} %param.13), kind=kOutput, calls=%fused_computation.12 | convolution fusion | flops 201326592 | bytes 12812288 | tf_op jit(solution)/shard_map/dot_general | solution.py:16
  199.2 12.2 %fusion.24 = bf16[16,3072]{1,0:T(8,128)(2,1)} fusion(bf16[1,1,2048,3072]{3,2,1,0:T(8,128)(2,1)} %param.15, bf16[16,3072]{1,0:T(8,128)(2,1)S(1)} %reshape.161, bf16[1,1,3072,2048]{3,2,1,0:T(8,128)(2,1)} %param.14, f32[16,2048]{1,0:T(8,128)S(1)} %fusion.12), kind=kOutput, calls=%fused_computation.20 | convolution fusion | flops 402898944 | bytes 25493504 | tf_op jit(solution)/shard_map/dot_general | solution.py:49
  211.5 33.9 %all-reduce.11.cloned.1.call-done = bf16[16,3072]{1,0:T(8,128)(2,1)} async-done(((bf16[16,3072]{1,0:T(8,128)(2,1)}), bf16[16,3072]{1,0:T(8,128)(2,1)}) %all-reduce.11.cloned.1.call-update) | async-done | bytes 98320
  246.3 3.7 %all_to_all.33 = bf16[2,2,3072]{2,1,0:T(2,128)(2,1)S(1)} all-to-all(bf16[2,2,3072]{2,1,0:T(2,128)(2,1)S(1)} %reshape.153), channel_id=1, replica_groups=mesh['groups'=2,'section'=2,'expert'=4,'pair'=2] {'pair'}, dimensions={0} | all-to-all | bytes 49152 | tf_op jit(solution)/shard_map/all_to_all | solution.py:55
  250.3 1.5 collective-permute-start.5
  251.8 2.2 collective-permute-done.5
  (72 shorter events, 7.4 us)
Async XLA Ops:
  7.2 42.3 %copy-start = (bf16[1,3072,2]{1,2,0:T(2,128)(2,1)S(1)}, bf16[1,3072,2]{1,2,0:T(2,128)(2,1)}, u32[]{:S(2)}) copy-start(bf16[1,3072,2]{1,2,0:T(2,128)(2,1)} %param.12) | copy-start | bytes 36868
  7.2 76.9 %all-reduce.7.cloned.1.call-start = ((), (), s32[]{:S(2)}) async-start(), calls=%async_computation.6 | async-start | bytes 196608
  7.2 83.4 %collective-permute-start = (bf16[2,3072]{1,0:T(2,128)(2,1)}, bf16[2,3072]{1,0:T(2,128)(2,1)S(1)}, u32[]{:S(2)}, u32[]{:S(2)}) collective-permute-start(bf16[2,3072]{1,0:T(2,128)(2,1)} %bitcast.139), channel_id=1, source_target_pairs={{8,0},{0,8},{9,1},{1,9},{10,2},{2,10},{11,3},{3,11},{12,4},{4,12},... | collective-permute-start | bytes 36872 | tf_op jit(solution)/shard_map/ppermute | solution.py:12
  37.1 12.3 %copy-start.2 = (s32[1,3,2,1]{1,3,2,0:T(1,128)S(1)}, s32[1,3,2,1]{1,3,2,0:T(1,128)}, u32[]{:S(2)}) copy-start(s32[1,3,2,1]{1,3,2,0:T(1,128)} %param.10) | copy-start | bytes 76
  37.1 12.3 %copy-start.1 = (f32[1,3072]{1,0:T(1,128)S(1)}, f32[1,3072]{1,0:T(1,128)}, u32[]{:S(2)}) copy-start(f32[1,3072]{1,0:T(1,128)} %param.11) | copy-start | bytes 36868
  37.1 12.4 %copy-start.3 = (bf16[1,2,3072]{2,1,0:T(2,128)(2,1)S(1)}, bf16[1,2,3072]{2,1,0:T(2,128)(2,1)}, u32[]{:S(2)}) copy-start(bf16[1,2,3072]{2,1,0:T(2,128)(2,1)} %param.8) | copy-start | bytes 36868
  37.1 13.0 %copy-start.4 = (u32[32]{0:T(128)S(1)}, u32[32]{0:T(128)}, u32[]{:S(2)}) copy-start(u32[32]{0:T(128)} %constant.44) | copy-start | bytes 388
  88.9 3.8 %collective-permute-start.1 = (bf16[2,3072]{1,0:T(2,128)(2,1)S(1)}, bf16[2,3072]{1,0:T(2,128)(2,1)S(1)}, u32[]{:S(2)}, u32[]{:S(2)}) collective-permute-start(bf16[2,3072]{1,0:T(2,128)(2,1)S(1)} %fusion.30), channel_id=1, source_target_pairs={{8,0},{0,8},{9,1},{1,9},{10,2},{2,10},{11,3},{3,11},{12,4},{4,12},... | collective-permute-start | bytes 36872 | tf_op jit(solution)/shard_map/ppermute | solution.py:12
  93.9 4.9 %all-to-all-start.2 = ((bf16[2,2,3072]{2,1,0:T(2,128)(2,1)}), bf16[2,2,3072]{2,1,0:T(2,128)(2,1)S(1)}, u32[]{:S(2)}, u32[]{:S(2)}) async-start(bf16[2,2,3072]{2,1,0:T(2,128)(2,1)} %reshape.147), calls=%async_computation.2 | async-start | bytes 49152 | tf_op jit(solution)/shard_map/all_to_all | solution.py:42
  97.2 67.7 %all-reduce.9.cloned.1.call-start = ((), (), s32[]{:S(2)}) async-start(), calls=%async_computation.7 | async-start | bytes 196608
  97.2 74.0 %collective-permute-start.3 = (bf16[2,3072]{1,0:T(2,128)(2,1)S(1)}, bf16[2,3072]{1,0:T(2,128)(2,1)S(1)}, u32[]{:S(2)}, u32[]{:S(2)}) collective-permute-start(bf16[2,3072]{1,0:T(2,128)(2,1)S(1)} %broadcast_select_fusion.4), channel_id=1, source_target_pairs={{8,0},{0,8},{9,1},{1,9},{10,2},{2,10},{11,3},{3,11},{12,4},{4,12},... | collective-permute-start | bytes 36872 | tf_op jit(solution)/shard_map/ppermute | solution.py:12
  169.7 3.8 %collective-permute-start.2 = (bf16[2,3072]{1,0:T(2,128)(2,1)S(1)}, bf16[2,3072]{1,0:T(2,128)(2,1)S(1)}, u32[]{:S(2)}, u32[]{:S(2)}) collective-permute-start(bf16[2,3072]{1,0:T(2,128)(2,1)S(1)} %fusion.31), channel_id=1, source_target_pairs={{8,0},{0,8},{9,1},{1,9},{10,2},{2,10},{11,3},{3,11},{12,4},{4,12},... | collective-permute-start | bytes 36872 | tf_op jit(solution)/shard_map/ppermute | solution.py:12
  174.7 4.9 %all-to-all-start.4 = ((bf16[2,2,3072]{2,1,0:T(2,128)(2,1)}), bf16[2,2,3072]{2,1,0:T(2,128)(2,1)S(1)}, u32[]{:S(2)}, u32[]{:S(2)}) async-start(bf16[2,2,3072]{2,1,0:T(2,128)(2,1)} %reshape.151), calls=%async_computation.4 | async-start | bytes 49152 | tf_op jit(solution)/shard_map/all_to_all | solution.py:42
  177.9 67.5 %all-reduce.11.cloned.1.call-start = ((), (), s32[]{:S(2)}) async-start(), calls=%async_computation.8 | async-start | bytes 196608
  178.0 73.8 %collective-permute-start.4 = (bf16[2,3072]{1,0:T(2,128)(2,1)S(1)}, bf16[2,3072]{1,0:T(2,128)(2,1)S(1)}, u32[]{:S(2)}, u32[]{:S(2)}) collective-permute-start(bf16[2,3072]{1,0:T(2,128)(2,1)S(1)} %broadcast_select_fusion.3), channel_id=1, source_target_pairs={{8,0},{0,8},{9,1},{1,9},{10,2},{2,10},{11,3},{3,11},{12,4},{4,12},... | collective-permute-start | bytes 36872 | tf_op jit(solution)/shard_map/ppermute | solution.py:12
  250.3 3.8 %collective-permute-start.5 = (bf16[2,3072]{1,0:T(2,128)(2,1)S(1)}, bf16[2,3072]{1,0:T(2,128)(2,1)S(1)}, u32[]{:S(2)}, u32[]{:S(2)}) collective-permute-start(bf16[2,3072]{1,0:T(2,128)(2,1)S(1)} %fusion.32), channel_id=1, source_target_pairs={{8,0},{0,8},{9,1},{1,9},{10,2},{2,10},{11,3},{3,11},{12,4},{4,12},... | collective-permute-start | bytes 36872 | tf_op jit(solution)/shard_map/ppermute | solution.py:12
Sparse Core Ops, SparseCore 0:
  49.5 34.5 all-reduce.6
  130.9 33.9 all-reduce.8
  211.5 33.9 all-reduce.10
where the time goes:
time: 262 us; the launch traced here: 261 us
  waiting for transfers between devices  107 us (41%)
  matrix products  58.1 us (22%)
  blocking collectives  55.2 us (21%)
  starting transfers between devices  17.3 us (7%)
  between operations  14.7 us (6%)
  local copies, waits for them, and re-layouts  5.53 us (2%)
  other arithmetic  3.53 us (1%)
    unnamed x6, waiting for transfers between devices  100 us
    all_gather x3, blocking collectives, moe_layer(): lax.all_gather(arrived.reshape(slots_all, width), 'expert', axis=0, tiled...  40.2 us
    dot_general x3, matrix products, moe_layer(): jnp.dot(hidden, down_w, preferred_element_type=jnp.float32)  36.5 us
    dot_general x3, matrix products, expand(): gate = jnp.dot(rows, gate_w, preferred_element_type=jnp.float32)  18.9 us
    all_to_all x3, blocking collectives, moe_layer(): lax.all_to_all(answer, 'pair', split_axis=0, concat_axis=0, tiled=True)  11.2 us
    ppermute x6, starting transfers between devices, shifted(): return lax.ppermute(block, axis, route)  10.7 us
    all_to_all x2, starting transfers between devices, moe_layer(): lax.all_to_all(parcel, 'pair', split_axis=0, concat_axis=0, tiled=True)  6.49 us
    ppermute x6, waiting for transfers between devices, shifted(): return lax.ppermute(block, axis, route)  6.48 us
  transfers between devices with their start and end apart: 11, of which 6 were waited for; matrix products, arithmetic and copies ran while one was open for 24% of the time, Pallas kernels for 0%

commit v1 on v0

v1 whole, which is shorter than its diff:
```python
import functools

import jax
import jax.numpy as jnp
from jax import lax
from jax.experimental import pallas as pl
from jax.experimental.pallas import tpu as pltpu
from jax.sharding import PartitionSpec as P

EPSILON = 1e-06
F32 = jnp.float32
BF16 = jnp.bfloat16


def width_of(total, most):
    width = most
    while total % width:
        width -= 128
    return width


def window_kernel(
    sizes, act, queue, picks, gain, table, gate_hbm, up_hbm, down_hbm, inflight, finished, *scratch
):
    sections, experts_ax, pairs, ticks, tok, width, hidden_w, fw, dw, levels, pads = sizes
    n = experts_ax * pairs
    fc, dc = hidden_w // fw, width // dw
    it = iter(scratch)
    gate_w, up_w, down_w, w_sem = next(it), next(it), next(it), next(it)
    queue_in, q_send, q_recv = next(it), next(it), next(it)
    held, h_send, h_recv = next(it), next(it), next(it)
    end_now, end_side, end_send, end_recv = next(it), next(it), next(it), next(it)
    per_level = [tuple(next(it) for _ in range(11)) for _ in range(levels)]
    sec = lax.axis_index("section")
    my_e = lax.axis_index("expert")
    my_p = lax.axis_index("pair")
    me = my_e * pairs + my_p

    def fetch(kind, c):
        if kind == 0:
            src, dst = gate_hbm.at[0, 0, :, pl.ds(c * fw, fw)], gate_w.at[c]
        elif kind == 1:
            src, dst = up_hbm.at[0, 0, :, pl.ds(c * fw, fw)], up_w.at[c]
        else:
            src, dst = down_hbm.at[0, 0, :, pl.ds(c * dw, dw)], down_w.at[c]
        base = (0, fc, 2 * fc)[kind]
        return pltpu.make_async_copy(src, dst, w_sem.at[base + c])

    for c in range(fc):
        fetch(0, c).start()
        fetch(1, c).start()
    for c in range(dc):
        fetch(2, c).start()

    def peer_at(off):
        peer = lax.rem(me + off, n)
        return peer, {"expert": peer // pairs, "pair": lax.rem(peer, pairs)}

    barrier = pltpu.get_barrier_semaphore()

    def greet(off, carry):
        pl.semaphore_signal(barrier, inc=1, device_id=peer_at(off)[1])
        return carry

    lax.fori_loop(1, n, greet, 0)
    for off in range(1, sections):
        pl.semaphore_signal(barrier, inc=1, device_id={"section": lax.rem(sec + off, sections)})
    pl.semaphore_wait(barrier, n - 1 + sections - 1)

    for k in range(1, ticks):
        origin = sections - k
        if origin == 0:
            continue
        copy = pltpu.make_async_remote_copy(
            queue.at[0],
            queue_in.at[k - 1],
            q_send.at[k - 1],
            q_recv.at[k - 1],
            device_id={"section": 0},
        )

        @pl.when(sec == origin)
        def _():
            copy.start()

    def final_spot(k):
        place = ticks - 1 - k
        return (0, True) if place == sections else (place, False)

    movers = []
    if ticks <= sections:
        movers.append((sections - ticks, 0, True))
    for s in range(ticks, sections):
        movers.append((s - ticks, s, False))
    for origin, goal, now in movers:
        dst = end_now if now else end_side
        sem = 0 if now else 1
        if origin == goal:

            @pl.when(sec == origin)
            def _():
                dst[...] = queue[0]

        else:

            @pl.when(sec == origin)
            def _():
                pltpu.make_async_remote_copy(
                    queue.at[0],
                    dst,
                    end_send.at[2],
                    end_recv.at[sem],
                    device_id={"section": goal},
                ).start()

    rows_pick = lax.broadcasted_iota

    def level_work(level):
        count = ticks - level
        real = count * tok
        rows = pads[level]
        (x_send, xs_sem, xr_sem, x_all, lhs, h_all, p_send, ps_sem, pr_sem, p_all, res) = per_level[
            level
        ]
        if level == 0:
            blocks = [act[0].astype(F32)]
            for k in range(1, ticks):
                if sections - k == 0:
                    blocks.append(queue[0].astype(F32))
                else:

                    @pl.when(sec == 0)
                    def _():
                        pltpu.make_async_remote_copy(
                            queue.at[0],
                            queue_in.at[k - 1],
                            q_send.at[k - 1],
                            q_recv.at[k - 1],
                            device_id={"section": 1},
                        ).wait_recv()

                    @pl.when(sec != 0)
                    def _():
                        queue_in[k - 1] = jnp.zeros((tok, width), BF16)

                    blocks.append(queue_in[k - 1].astype(F32))
        else:
            for i in range(count):
                k = level + i

                def arrive():
                    pltpu.make_async_remote_copy(
                        res.at[i],
                        held.at[level - 1, i],
                        h_send.at[level - 1, i],
                        h_recv.at[level - 1, i],
                        device_id={"section": 0},
                    ).wait_recv()

                def blank():
                    held[level - 1, i] = jnp.zeros((tok, width), BF16)

                if i == 0:
                    arrive()
                else:
                    pl.when(sec == level)(arrive)
                    pl.when(sec != level)(blank)
            blocks = [held[level - 1, i].astype(F32) for i in range(count)]
        if rows > real:
            blocks.append(jnp.zeros((rows - real, width), F32))
        wide = jnp.concatenate(blocks, axis=0)
        square = jnp.mean(wide * wide, axis=-1, keepdims=True)
        normed = (wide * lax.rsqrt(square + EPSILON) * gain[...]).astype(BF16).astype(F32)
        tab = table[0].astype(F32)
        first = jnp.sum(normed * tab[0:1], axis=-1, keepdims=True)
        second = jnp.sum(normed * tab[1:2], axis=-1, keepdims=True)
        line = rows_pick(jnp.int32, (rows, 1), 0)
        pick = jnp.zeros((rows, 1), jnp.int32)
        for i in range(count):
            for t in range(tok):
                pick = jnp.where(line == i * tok + t, picks[0, level + i, t, 0], pick)
        delta = jnp.where(pick == 0, first - second, second - first)
        weight = 1.0 / (1.0 + jnp.exp(-delta))
        for p in range(pairs):
            x_send[p] = jnp.where(pick == p, normed, 0.0).astype(BF16)

        def x_copy(slot, peer, target):
            return pltpu.make_async_remote_copy(
                x_send.at[slot],
                x_all.at[me],
                xs_sem.at[peer],
                xr_sem.at[me],
                device_id=target,
            )

        def send_x(off, carry):
            peer, target = peer_at(off)
            x_copy(lax.rem(peer, pairs), peer, target).start()
            return carry

        lax.fori_loop(1, n, send_x, 0)
        x_all[me] = x_send[my_p]

        def take_x(off, carry):
            peer, target = peer_at(off)
            pltpu.make_async_remote_copy(
                x_send.at[0], x_all.at[peer], xs_sem.at[peer], xr_sem.at[peer], device_id=target
            ).wait_recv()
            return carry

        lax.fori_loop(1, n, take_x, 0)
        if rows % 8 == 0:
            lhs[...] = x_all[...].astype(F32).reshape(n * rows, width).astype(BF16)
        else:
            group = max(1, 16 // rows)
            for d in range(0, n, group):
                lhs[d * rows : (d + group) * rows] = jnp.concatenate(
                    [x_all[d + j].astype(F32) for j in range(group)], axis=0
                ).astype(BF16)

        def widen(c, carry):
            if level == 0:
                fetch(0, c).wait()
                fetch(1, c).wait()
            gate = jnp.dot(lhs[...], gate_w[c], preferred_element_type=F32)
            upper = jnp.dot(lhs[...], up_w[c], preferred_element_type=F32)
            h_all[c] = (gate / (1.0 + jnp.exp(-gate)) * upper).astype(BF16)
            return carry

        lax.fori_loop(0, fc, widen, 0)

        def p_copy(c, peer, target):
            return pltpu.make_async_remote_copy(
                p_send.at[c, peer],
                p_all.at[c, me],
                ps_sem.at[c, peer],
                pr_sem.at[c, me],
                device_id=target,
            )

        def narrow(c, carry):
            if level == 0:
                fetch(2, c).wait()
            part = jnp.zeros((n * rows, dw), F32)
            for i in range(fc):
                part = part + jnp.dot(
                    h_all[i], down_w[c, i * fw : (i + 1) * fw], preferred_element_type=F32
                )
            if rows % 8 == 0:
                p_send[c] = part.reshape(n, rows, dw).astype(BF16)
            else:
                for d in range(n):
                    p_send[c, d] = part[d * rows : (d + 1) * rows].astype(BF16)

            def send_p(off, inner):
                peer, target = peer_at(off)
                p_copy(c, peer, target).start()
                return inner

            lax.fori_loop(1, n, send_p, 0)
            p_all[c, me] = p_send[c, me]
            return carry

        lax.fori_loop(0, dc, narrow, 0)
        for c in range(dc):

            def take_p(off, carry):
                peer, target = peer_at(off)
                pltpu.make_async_remote_copy(
                    p_send.at[c, peer],
                    p_all.at[c, peer],
                    ps_sem.at[c, peer],
                    pr_sem.at[c, peer],
                    device_id=target,
                ).wait_recv()
                return carry

            lax.fori_loop(1, n, take_p, 0)
            total = jnp.sum(p_all[c].astype(F32), axis=0).astype(BF16).astype(F32)
            span = slice(c * dw, (c + 1) * dw)
            done = wide[:, span] + weight * total
            for i in range(count):
                res[i, :, span] = done[i * tok : (i + 1) * tok].astype(BF16)

        def goals(i):
            k = level + i
            place, now = final_spot(k)
            out = []
            if i == 0:
                middle = (sec >= level) & (sec < sections - 1)
            else:
                middle = (sec == level) & (sec < sections - 1)
            target = {"section": lax.rem(sec + 1, sections)}
            if k < ticks - 1:
                if level + 1 < levels:
                    out.append(
                        (
                            middle,
                            pltpu.make_async_remote_copy(
                                res.at[i],
                                held.at[level, i],
                                h_send.at[level, i],
                                h_recv.at[level, i],
                                device_id=target,
                            ),
                        )
                    )
            else:
                out.append(
                    (
                        middle,
                        pltpu.make_async_remote_copy(
                            res.at[i], end_now, h_send.at[level, i], end_recv.at[0], device_id=target
                        ),
                    )
                )
            if i == 0 or level == sections - 1:
                last = sec == sections - 1
                dst, sem = (end_now, 0) if now else (end_side, 1)
                if place == sections - 1 and not now:
                    out.append((last, None))
                else:
                    out.append(
                        (
                            last,
                            pltpu.make_async_remote_copy(
                                res.at[i],
                                dst,
                                h_send.at[level, i],
                                end_recv.at[sem],
                                device_id={"section": place},
                            ),
                        )
                    )
            return out

        for i in range(count):
            for condition, copy in goals(i):

                @pl.when(condition)
                def _():
                    if copy is None:
                        end_side[...] = res[i]
                    else:
                        copy.start()

        def settle(off, carry):
            peer, target = peer_at(off)
            x_copy(0, peer, target).wait_send()
            for c in range(dc):
                p_copy(c, peer, target).wait_send()
            return carry

        def finish():
            lax.fori_loop(1, n, settle, 0)
            for i in range(count):
                for condition, copy in goals(i):
                    if copy is not None:

                        @pl.when(condition)
                        def _():
                            copy.wait_send()

        return finish

    for level in range(levels):
        if level == 0:
            level_work(0)()
        else:

            @pl.when(sec >= level)
            def _():
                level_work(level)()

    for k in range(1, ticks):
        origin = sections - k
        if origin == 0:
            continue

        @pl.when(sec == origin)
        def _():
            pltpu.make_async_remote_copy(
                queue.at[0],
                queue_in.at[k - 1],
                q_send.at[k - 1],
                q_recv.at[k - 1],
                device_id={"section": 0},
            ).wait_send()

    for origin, goal, now in movers:
        if origin != goal:

            @pl.when(sec == origin)
            def _():
                pltpu.make_async_remote_copy(
                    queue.at[0],
                    end_now,
                    end_send.at[2],
                    end_recv.at[0],
                    device_id={"section": goal},
                ).wait_send()

    def land(dst, sem):
        pltpu.make_async_remote_copy(
            queue.at[0], dst, end_send.at[0], end_recv.at[sem], device_id={"section": 0}
        ).wait_recv()

    local_now = [goal for origin, goal, now in movers if now and origin == goal]
    if not local_now:
        land(end_now, 0)
    else:
        pl.when(sec != local_now[0])(lambda: land(end_now, 0))
    local_side = [goal for origin, goal, now in movers if not now and origin == goal]
    if ticks >= sections:
        local_side.append(sections - 1)
    remote = sec >= 0
    for goal in local_side:
        remote = remote & (sec != goal)
    pl.when(remote)(lambda: land(end_side, 1))
    inflight[0] = end_now[...]
    finished[0] = end_side[...]


def body(act, queue, picks, gain, table, gate_w, up_w, down_w):
    sections, experts_ax, pairs = (lax.axis_size(a) for a in ("section", "expert", "pair"))
    ticks, tok = picks.shape[1], picks.shape[2]
    width, hidden_w = gate_w.shape[2], gate_w.shape[3]
    n = experts_ax * pairs
    fw, dw = width_of(hidden_w, 512), width_of(width, 768)
    fc, dc = hidden_w // fw, width // dw
    levels = min(sections, ticks)
    assert ticks <= sections + 1
    pads = []
    for level in range(levels):
        real = (ticks - level) * tok
        pads.append(real if real in (1, 2, 4) else -(-real // 8) * 8)
    dma = pltpu.SemaphoreType.DMA
    vm = pltpu.VMEM
    scratch = [
        vm((fc, width, fw), BF16),
        vm((fc, width, fw), BF16),
        vm((dc, hidden_w, dw), BF16),
        dma((2 * fc + dc,)),
        vm((ticks, tok, width), BF16),
        dma((ticks,)),
        dma((ticks,)),
        vm((levels, ticks, tok, width), BF16),
        dma((levels, ticks)),
        dma((levels, ticks)),
        vm((tok, width), BF16),
        vm((tok, width), BF16),
        dma((3,)),
        dma((2,)),
    ]
    for level in range(levels):
        rows = pads[level]
        scratch += [
            vm((pairs, rows, width), BF16),
            dma((n,)),
            dma((n,)),
            vm((n, rows, width), BF16),
            vm((n * rows, width), BF16),
            vm((fc, n * rows, fw), BF16),
            vm((dc, n, rows, dw), BF16),
            dma((dc, n)),
            dma((dc, n)),
            vm((dc, n, rows, dw), BF16),
            vm((ticks - level, tok, width), BF16),
        ]
    sizes = (
        sections, experts_ax, pairs, ticks, tok, width, hidden_w, fw, dw, levels, tuple(pads)
    )
    in_vmem = pl.BlockSpec(memory_space=pltpu.VMEM)
    anywhere = pl.BlockSpec(memory_space=pl.ANY)
    return pl.pallas_call(
        functools.partial(window_kernel, sizes),
        out_shape=(
            jax.ShapeDtypeStruct(act.shape, BF16),
            jax.ShapeDtypeStruct(act.shape, BF16),
        ),
        in_specs=[
            in_vmem,
            in_vmem,
            pl.BlockSpec(memory_space=pltpu.SMEM),
            in_vmem,
            in_vmem,
            anywhere,
            anywhere,
            anywhere,
        ],
        out_specs=(in_vmem, in_vmem),
        scratch_shapes=scratch,
        compiler_params=pltpu.CompilerParams(
            collective_id=0, has_side_effects=True, vmem_limit_bytes=60 * 1024 * 1024
        ),
    )(act, queue, picks, gain, jnp.swapaxes(table, 1, 2), gate_w, up_w, down_w)


def solution(mesh):
    in_specs = (
        P("section", ("groups", "expert", "pair"), None),
        P("section", ("groups", "expert", "pair"), None),
        P("section", None, ("groups", "expert", "pair"), None),
        P("section", None),
        P("section", None, None),
        P("section", "pair", None, "expert"),
        P("section", "pair", None, "expert"),
        P("section", "pair", "expert", None),
    )
    out_specs = (
        P("section", ("groups", "expert", "pair"), None),
        P("section", ("groups", "expert", "pair"), None),
    )
    return jax.shard_map(body, mesh=mesh, in_specs=in_specs, out_specs=out_specs, check_vma=False)
```

time: 262 us -> 62.6 us (0.24)
  waiting for transfers between devices: 107 us -> 0 us
  matrix products: 58.1 us -> 0 us
  Pallas kernels: 0 us -> 57.6 us
  blocking collectives: 55.2 us -> 0 us
  starting transfers between devices: 17.3 us -> 0 us
  between operations: 14.7 us -> 0.64 us
  other arithmetic: 3.53 us -> 0 us
    unnamed x6 -> x0, waiting for transfers between devices: 100 us -> none
    dot_general x15 -> x0, matrix products: 58.1 us -> none  [the longest x3 36.5 us: moe_layer(): jnp.dot(hidden, down_w, preferred_element_type=jnp.float32)]
    pallas_call x0 -> x1, Pallas kernels: none -> 57.6 us  [body(): pl.pallas_call(functools.partial(window_kernel, sizes), out_shape=(jax.Sh...]
    all_gather x3 -> x0, blocking collectives: 40.2 us -> none  [moe_layer(): lax.all_gather(arrived.reshape(slots_all, width), 'expert', axis=0, tiled...]
    all_to_all x4 -> x0, blocking collectives: 14.9 us -> none  [the longest x3 11.2 us: moe_layer(): lax.all_to_all(answer, 'pair', split_axis=0, concat_axis=0, tiled=True)]
    ppermute x6 -> x0, starting transfers between devices: 10.7 us -> none  [shifted(): return lax.ppermute(block, axis, route)]
    all_to_all x2 -> x0, starting transfers between devices: 6.49 us -> none  [moe_layer(): lax.all_to_all(parcel, 'pair', split_axis=0, concat_axis=0, tiled=True)]
    ppermute x6 -> x0, waiting for transfers between devices: 6.48 us -> none  [shifted(): return lax.ppermute(block, axis, route)]
  transfers between devices with their start and end apart: 11 -> 0, of which waited for: 6 -> 0; matrix products, arithmetic and copies ran while one was open for 24% -> 0% of each run, Pallas kernels for 0% -> 0%
where the time goes in v1:
time: 62.6 us; the launch traced here: 62.2 us
  Pallas kernels  57.6 us (92%)
  local copies, waits for them, and re-layouts  3.97 us (6%)
  between operations  0.64 us (1%)
    pallas_call x1, Pallas kernels, body(): pl.pallas_call(functools.partial(window_kernel, sizes), out_shape=(jax.Sh...  57.6 us
    unnamed x3, local copies, waits for them, and re-layouts  3.97 us

profile of v1, /device:TPU:0, one launch (start us, length us, event | category | flops | bytes accessed | tf_op | source)
XLA Modules:
  0.0 62.2 jit_solution(15847839458491218898)
XLA Ops:
  0.6 1.3 %copy.10.picks = s32[1,3,2,1]{3,2,1,0:T(2,128)} copy(s32[1,3,2,1]{1,3,2,0:T(1,128)} %param.10) | data formatting | bytes 48 | tf_op args[2]
  2.0 57.6 %shard_map.95 = (bf16[1,2,3072]{2,1,0:T(2,128)(2,1)}, bf16[1,2,3072]{2,1,0:T(2,128)(2,1)}) custom-call(bf16[1,2,3072]{2,1,0:T(2,128)(2,1)} %act.1, bf16[1,2,3072]{2,1,0:T(2,128)(2,1)} %queue.1, s32[1,3,2,1]{3,2,1,0:T(2,128)} %copy.10.picks, f32[1,3072]{1,0:T(1,128)} %gain.1, bf16[1,2,3072]{2,1,0:T(2,128)(2,1)} %bitcast.1, ...), custom_call_target="tpu_custom_call" | custom-call | tf_op jit(solution)/shard_map/pallas_call | solution.py:475
  59.5 1.3 %copy.13 = bf16[1,2,3072]{2,1,0:T(2,128)(2,1)} copy(bf16[1,2,3072]{2,1,0:T(2,128)(2,1)} %get-tuple-element.4) | data formatting | bytes 24576
  60.9 1.3 %copy.14 = bf16[1,2,3072]{2,1,0:T(2,128)(2,1)} copy(bf16[1,2,3072]{2,1,0:T(2,128)(2,1)} %get-tuple-element.5) | data formatting | bytes 24576

commit v2 on v0

v2 whole, which is shorter than its diff:
```python
import functools

import jax
import jax.numpy as jnp
from jax import lax
from jax.experimental import pallas as pl
from jax.experimental.pallas import tpu as pltpu
from jax.sharding import PartitionSpec as P

EPSILON = 1e-06
F32 = jnp.float32
BF16 = jnp.bfloat16


def width_of(total, most):
    width = most
    while total % width:
        width -= 128
    return width


def window_kernel(
    sizes, act, queue, picks, gain, table, gate_hbm, up_hbm, down_hbm, inflight, finished, *scratch
):
    sections, chips, pairs, ticks, tok, width, hidden_w, fw, dw, levels = sizes
    fc, dc = hidden_w // fw, width // dw
    wide_row = width + 128
    it = iter(scratch)
    gate_w, up_w, down_w, w_sem = next(it), next(it), next(it), next(it)
    queue_in, q_send, q_recv = next(it), next(it), next(it)
    end_send, end_recv = next(it), next(it)
    last = tuple(next(it) for _ in range(6))
    per_level = [tuple(next(it) for _ in range(22)) for _ in range(levels)]
    sec = lax.axis_index("section")
    my_e = lax.axis_index("expert")
    my_p = lax.axis_index("pair")

    def fetch(kind, c):
        if kind == 0:
            src, dst = gate_hbm.at[0, 0, :, pl.ds(c * fw, fw)], gate_w.at[c]
        elif kind == 1:
            src, dst = up_hbm.at[0, 0, :, pl.ds(c * fw, fw)], up_w.at[c]
        else:
            src, dst = down_hbm.at[0, 0, :, pl.ds(c * dw, dw)], down_w.at[c]
        base = (0, fc, 2 * fc)[kind]
        return pltpu.make_async_copy(src, dst, w_sem.at[base + c])

    def next_section(off=1):
        return lax.rem(sec + off, sections)

    barrier = pltpu.get_barrier_semaphore()

    def greet(off, carry):
        pl.semaphore_signal(
            barrier,
            inc=1,
            device_id={
                "section": lax.rem(sec + off // chips, sections),
                "expert": lax.rem(my_e + lax.rem(off, chips), chips),
            },
        )
        return carry

    lax.fori_loop(1, sections * chips, greet, 0)
    for q in range(1, pairs):
        pl.semaphore_signal(barrier, inc=1, device_id={"pair": lax.rem(my_p + q, pairs)})
    for c in range(fc):
        fetch(0, c).start()
        fetch(1, c).start()
    for c in range(dc):
        fetch(2, c).start()
    pl.semaphore_wait(barrier, sections * chips - 1 + pairs - 1)

    def queue_copy(k):
        return pltpu.make_async_remote_copy(
            queue.at[0],
            queue_in.at[k - 1],
            q_send.at[k - 1],
            q_recv.at[k - 1],
            device_id={"section": 0},
        )

    for k in range(1, ticks):
        if sections - k > 0:
            pl.when(sec == sections - k)(queue_copy(k).start)

    movers = []
    if ticks <= sections:
        movers.append((sections - ticks, 0, True))
    for s in range(ticks, sections):
        movers.append((s - ticks, s, False))

    def mover_copy(goal, now):
        return pltpu.make_async_remote_copy(
            queue.at[0],
            end_recv_rows.at[0 if now else 1],
            end_send.at[0],
            end_recv.at[0 if now else 1],
            device_id={"section": goal},
        )

    end_recv_rows = next(it)
    for origin, goal, now in movers:
        if origin != goal:
            pl.when(sec == origin)(mover_copy(goal, now).start)

    def routes(level, i):
        k = level + i
        out = []
        if level <= sections - 2:
            fits = (sec >= level) if i == 0 else (sec == level)
            out.append((fits & (sec < sections - 1), False, next_section(), False))
        if i == 0 or level == sections - 1:
            place = ticks - 1 - k
            out.append(
                (sec == sections - 1, True, place % sections, place == sections - 1)
            )
        return out

    def slots(level, i, to_last):
        if to_last:
            return last, level + i
        return per_level[level][16:22], i

    def rest_copies(level, i, to_last, place, x_ref):
        w_out, r_send = per_level[level][12], per_level[level][13]
        (_, xs, ws, _, x_sem, weight_sem), at = slots(level, i, to_last)
        return (
            pltpu.make_async_remote_copy(
                x_ref, xs.at[at], r_send.at[i, 0], x_sem.at[at], device_id={"section": place}
            ),
            pltpu.make_async_remote_copy(
                w_out.at[i], ws.at[at], r_send.at[i, 1], weight_sem.at[at],
                device_id={"section": place},
            ),
        )

    def z_copy(level, i, c, j, to_last, place):
        z_send, z_sem = per_level[level][14], per_level[level][15]
        (parts, _, _, part_sem, _, _), at = slots(level, i, to_last)
        return pltpu.make_async_remote_copy(
            z_send.at[i, c, j],
            parts.at[at, c, my_e],
            z_sem.at[i, c, j],
            part_sem.at[at, c, my_e],
            device_id={"section": place, "expert": j},
        )

    def combine(bufs, at, own, store):
        parts, xs, ws, part_sem, x_sem, weight_sem = bufs
        aside = {"section": next_section()}
        if not own:
            pltpu.make_async_remote_copy(
                xs.at[at], xs.at[at], end_send.at[1], x_sem.at[at], device_id=aside
            ).wait_recv()
            pltpu.make_async_remote_copy(
                ws.at[at], ws.at[at], end_send.at[1], weight_sem.at[at], device_id=aside
            ).wait_recv()
        for c in range(dc):

            def take(off, carry):
                j = lax.rem(my_e + off, chips)
                pltpu.make_async_remote_copy(
                    parts.at[at, c, j],
                    parts.at[at, c, j],
                    end_send.at[1],
                    part_sem.at[at, c, j],
                    device_id=aside,
                ).wait_recv()
                return carry

            lax.fori_loop(1 if own else 0, chips, take, 0)
            total = jnp.sum(parts[at, c].astype(F32), axis=0).astype(BF16).astype(F32)
            span = slice(c * dw, (c + 1) * dw)
            done = xs[at, :, span].astype(F32) + ws[at][:, 0:1] * total
            store(span, done.astype(BF16))

    def level_work(level):
        count = ticks - level
        real = count * tok
        pad = -(-real // 8) * 8
        half = count * chips * tok
        (
            x_in, x_send, x_all, xs_sem, xf_sem, xr_sem, lhs, h_all, s_buf, d_buf, ds_sem, dr_sem,
            w_out, r_send, z_send, z_sem,
        ) = per_level[level][:16]
        if level == 0:
            x_in[0] = act[0]
            for k in range(1, ticks):
                if sections - k == 0:
                    x_in[k] = queue[0]
                else:

                    @pl.when(sec == 0)
                    def _():
                        queue_copy(k).wait_recv()
                        x_in[k] = queue_in[k - 1]

                    @pl.when(sec != 0)
                    def _():
                        x_in[k] = jnp.zeros((tok, width), BF16)

        else:
            for i in range(count):

                def arrive():
                    def store(span, rows):
                        x_in[i, :, span] = rows

                    combine(per_level[level - 1][16:22], i, False, store)

                if i == 0:
                    arrive()
                else:
                    pl.when(sec == level)(arrive)

                    @pl.when(sec != level)
                    def _():
                        x_in[i] = jnp.zeros((tok, width), BF16)

        blocks = [x_in[i].astype(F32) for i in range(count)]
        if pad > real:
            blocks.append(jnp.zeros((pad - real, width), F32))
        wide = jnp.concatenate(blocks, axis=0)
        square = jnp.mean(wide * wide, axis=-1, keepdims=True)
        normed = (wide * lax.rsqrt(square + EPSILON) * gain[...]).astype(BF16).astype(F32)
        line = lax.broadcasted_iota(jnp.int32, (pad, 1), 0)
        pick = jnp.zeros((pad, 1), jnp.int32)
        for i in range(count):
            for t in range(tok):
                pick = jnp.where(line == i * tok + t, picks[0, t, 0, level + i], pick)
        flag = jnp.broadcast_to(pick.astype(F32), (pad, 128))
        for i in range(count):
            x_send[i, :, 0:width] = normed[i * tok : (i + 1) * tok].astype(BF16)
            x_send[i, :, width:wide_row] = flag[i * tok : (i + 1) * tok].astype(BF16)

        def across(off):
            j = lax.rem(my_e + off, chips)
            return pltpu.make_async_remote_copy(
                x_send,
                x_all.at[my_e, my_p],
                xs_sem.at[j],
                xr_sem.at[my_e, my_p],
                device_id={"expert": j},
            )

        def beside(off, q):
            j = lax.rem(my_e + off, chips)
            return pltpu.make_async_remote_copy(
                x_send if isinstance(off, int) else x_all.at[j, my_p],
                x_all.at[j, my_p],
                xf_sem.at[j, q - 1],
                xr_sem.at[j, my_p],
                device_id={"pair": lax.rem(my_p + q, pairs)},
            )

        def arrived(j, p):
            pltpu.make_async_remote_copy(
                x_send, x_all.at[j, p], xs_sem.at[0], xr_sem.at[j, p],
                device_id={"section": next_section()},
            ).wait_recv()

        def go(off, carry):
            across(off).start()
            return carry

        lax.fori_loop(1, chips, go, 0)
        for q in range(1, pairs):
            beside(0, q).start()
        x_all[my_e, my_p] = x_send[...]
        tab = table[0].astype(F32)
        first = jnp.sum(normed * tab[0:1], axis=-1, keepdims=True)
        second = jnp.sum(normed * tab[1:2], axis=-1, keepdims=True)
        delta = jnp.where(pick == 0, first - second, second - first)
        weight = jnp.broadcast_to(1.0 / (1.0 + jnp.exp(-delta)), (pad, 128))
        for i in range(count):
            w_out[i] = weight[i * tok : (i + 1) * tok]

        def relay(off, carry):
            j = lax.rem(my_e + off, chips)
            arrived(j, my_p)
            for q in range(1, pairs):
                beside(off, q).start()
            return carry

        lax.fori_loop(1, chips, relay, 0)
        for i in range(count):
            for condition, to_last, place, own in routes(level, i):

                @pl.when(condition)
                def _():
                    if own:
                        bufs, at = slots(level, i, to_last)
                        bufs[1][at] = x_in[i]
                        bufs[2][at] = w_out[i]
                    else:
                        for copy in rest_copies(level, i, to_last, place, x_in.at[i]):
                            copy.start()

        def gather(off, carry):
            j = lax.rem(my_e + off, chips)
            for q in range(1, pairs):
                arrived(j, lax.rem(my_p + q, pairs))
            return carry

        lax.fori_loop(0, chips, gather, 0)
        order = [(p, i, e) for p in range(pairs) for i in range(count) for e in range(chips)]
        group = max(1, 16 // tok)
        for start in range(0, len(order), group):
            rows = jnp.concatenate(
                [x_all[e, p, i].astype(F32) for p, i, e in order[start : start + group]], axis=0
            )
            mine = rows[:, width : width + 1] == my_p.astype(F32)
            lhs[start * tok : (start + group) * tok] = jnp.where(
                mine, rows[:, 0:width], 0.0
            ).astype(BF16)

        def widen(c, carry):
            if level == 0:
                fetch(0, c).wait()
                fetch(1, c).wait()
            gate = jnp.dot(lhs[...], gate_w[c], preferred_element_type=F32)
            upper = jnp.dot(lhs[...], up_w[c], preferred_element_type=F32)
            h_all[c] = (gate / (1.0 + jnp.exp(-gate)) * upper).astype(BF16)
            return carry

        lax.fori_loop(0, fc, widen, 0)

        def trade(c, q):
            other = lax.rem(my_p + q, pairs)
            return pltpu.make_async_remote_copy(
                s_buf.at[c, other],
                d_buf.at[c, pairs - 1 - q],
                ds_sem.at[c, q - 1],
                dr_sem.at[c, pairs - 1 - q],
                device_id={"pair": other},
            )

        def send_parts(i, c):
            for condition, to_last, place, own in routes(level, i):

                def send(off, carry):
                    z_copy(level, i, c, lax.rem(my_e + off, chips), to_last, place).start()
                    return carry

                @pl.when(condition)
                def _():
                    if own:
                        bufs, at = slots(level, i, to_last)
                        bufs[0][at, c, my_e] = z_send[i, c, my_e]
                    lax.fori_loop(1 if own else 0, chips, send, 0)

        early = count if level == levels - 1 else count - 1

        def ship(c):
            total = s_buf[c, my_p].astype(F32)
            for q in range(1, pairs):
                trade(c, q).wait_recv()
            for q in range(1, pairs):
                total = total + d_buf[c, q - 1].astype(F32)
            for i in range(count):
                for e in range(chips):
                    at = (i * chips + e) * tok
                    z_send[i, c, e] = total[at : at + tok].astype(BF16)
            for i in range(early):
                send_parts(i, c)

        for c in range(dc):
            if level == 0:
                fetch(2, c).wait()
            part = jnp.dot(h_all[0], down_w[c, 0:fw], preferred_element_type=F32)
            for i in range(1, fc):
                part = part + jnp.dot(
                    h_all[i], down_w[c, i * fw : (i + 1) * fw], preferred_element_type=F32
                )
            for p in range(pairs):
                s_buf[c, p] = part[p * half : (p + 1) * half].astype(BF16)
            for q in range(1, pairs):
                trade(c, q).start()
            if c > 0:
                ship(c - 1)
        ship(dc - 1)
        for i in range(early, count):
            for c in range(dc):
                send_parts(i, c)

        def settle():
            def out(off, carry):
                across(off).wait_send()
                return carry

            lax.fori_loop(1, chips, out, 0)
            for q in range(1, pairs):

                def forwarded(off, carry):
                    beside(off, q).wait_send()
                    return carry

                beside(0, q).wait_send()
                lax.fori_loop(1, chips, forwarded, 0)
                for c in range(dc):
                    trade(c, q).wait_send()
            for i in range(count):
                for condition, to_last, place, own in routes(level, i):

                    @pl.when(condition)
                    def _():
                        if not own:
                            for copy in rest_copies(level, i, to_last, place, x_in.at[i]):
                                copy.wait_send()
                        for c in range(dc):

                            def sent(off, carry):
                                j = lax.rem(my_e + off, chips)
                                z_copy(level, i, c, j, to_last, place).wait_send()
                                return carry

                            lax.fori_loop(1 if own else 0, chips, sent, 0)

        return settle

    settles = []
    for level in range(levels):
        if level == 0:
            settles.append(level_work(0))
        else:

            @pl.when(sec >= level)
            def _():
                settles.append(level_work(level))

    def to_inflight(span, rows):
        inflight[0, :, span] = rows

    def to_finished(span, rows):
        finished[0, :, span] = rows

    for level in range(levels):
        if level > sections - 2:
            continue
        source = sec - 1
        fits = (source >= level) if level == ticks - 1 else (source == level)

        @pl.when(fits)
        def _():
            combine(per_level[level][16:22], ticks - 1 - level, False, to_inflight)

    for k in range(ticks):
        place = ticks - 1 - k

        @pl.when(sec == place % sections)
        def _():
            combine(last, k, place == sections - 1, to_inflight if place == sections else to_finished)

    for origin, goal, now in movers:
        target = inflight if now else finished
        if origin == goal:

            @pl.when(sec == origin)
            def _():
                target[0] = queue[0]

        else:

            @pl.when(sec == goal)
            def _():
                mover_copy(goal, now).wait_recv()
                target[0] = end_recv_rows[0 if now else 1]

            pl.when(sec == origin)(mover_copy(goal, now).wait_send)

    for k in range(1, ticks):
        if sections - k > 0:
            pl.when(sec == sections - k)(queue_copy(k).wait_send)
    for level in range(levels):
        if level == 0:
            settles[0]()
        else:
            pl.when(sec >= level)(settles[level])


def body(act, queue, picks, gain, table, gate_w, up_w, down_w):
    sections, experts_ax, pairs = (lax.axis_size(a) for a in ("section", "expert", "pair"))
    ticks, tok = picks.shape[1], picks.shape[2]
    width, hidden_w = gate_w.shape[2], gate_w.shape[3]
    fw, dw = width_of(hidden_w, 512), width_of(width, 768)
    fc, dc = hidden_w // fw, width // dw
    levels = min(sections, ticks)
    assert ticks <= sections + 1
    chips = experts_ax
    dma = pltpu.SemaphoreType.DMA
    vm = pltpu.VMEM

    def landing(count):
        return [
            vm((count, dc, chips, tok, dw), BF16),
            vm((count, tok, width), BF16),
            vm((count, tok, 128), F32),
            dma((count, dc, chips)),
            dma((count,)),
            dma((count,)),
        ]

    scratch = [
        vm((fc, width, fw), BF16),
        vm((fc, width, fw), BF16),
        vm((dc, hidden_w, dw), BF16),
        dma((2 * fc + dc,)),
        vm((ticks, tok, width), BF16),
        dma((ticks,)),
        dma((ticks,)),
        dma((2,)),
        dma((2,)),
    ] + landing(ticks)
    others = max(1, pairs - 1)
    for level in range(levels):
        count = ticks - level
        half = count * chips * tok
        scratch += [
            vm((count, tok, width), BF16),
            vm((count, tok, width + 128), BF16),
            vm((chips, pairs, count, tok, width + 128), BF16),
            dma((chips,)),
            dma((chips, others)),
            dma((chips, pairs)),
            vm((pairs * half, width), BF16),
            vm((fc, pairs * half, fw), BF16),
            vm((dc, pairs, half, dw), BF16),
            vm((dc, others, half, dw), BF16),
            dma((dc, others)),
            dma((dc, others)),
            vm((count, tok, 128), F32),
            dma((count, 2)),
            vm((count, dc, chips, tok, dw), BF16),
            dma((count, dc, chips)),
        ] + landing(count)
    scratch.append(vm((2, tok, width), BF16))
    sizes = (sections, chips, pairs, ticks, tok, width, hidden_w, fw, dw, levels)
    in_vmem = pl.BlockSpec(memory_space=pltpu.VMEM)
    anywhere = pl.BlockSpec(memory_space=pl.ANY)
    return pl.pallas_call(
        functools.partial(window_kernel, sizes),
        out_shape=(
            jax.ShapeDtypeStruct(act.shape, BF16),
            jax.ShapeDtypeStruct(act.shape, BF16),
        ),
        in_specs=[
            in_vmem,
            in_vmem,
            pl.BlockSpec(memory_space=pltpu.SMEM),
            in_vmem,
            in_vmem,
            anywhere,
            anywhere,
            anywhere,
        ],
        out_specs=(in_vmem, in_vmem),
        scratch_shapes=scratch,
        compiler_params=pltpu.CompilerParams(
            collective_id=0, has_side_effects=True, vmem_limit_bytes=60 * 1024 * 1024
        ),
    )(act, queue, jnp.transpose(picks, (0, 2, 3, 1)), gain, jnp.swapaxes(table, 1, 2), gate_w, up_w, down_w)


def solution(mesh):
    in_specs = (
        P("section", ("groups", "expert", "pair"), None),
        P("section", ("groups", "expert", "pair"), None),
        P("section", None, ("groups", "expert", "pair"), None),
        P("section", None),
        P("section", None, None),
        P("section", "pair", None, "expert"),
        P("section", "pair", None, "expert"),
        P("section", "pair", "expert", None),
    )
    out_specs = (
        P("section", ("groups", "expert", "pair"), None),
        P("section", ("groups", "expert", "pair"), None),
    )
    return jax.shard_map(body, mesh=mesh, in_specs=in_specs, out_specs=out_specs, check_vma=False)
```

time: 262 us -> 56.5 us (0.22)
  waiting for transfers between devices: 107 us -> 0 us
  matrix products: 58.1 us -> 0 us
  blocking collectives: 55.2 us -> 0 us
  Pallas kernels: 0 us -> 52.8 us
  starting transfers between devices: 17.3 us -> 0 us
  between operations: 14.7 us -> 0.64 us
  other arithmetic: 3.53 us -> 0 us
  local copies, waits for them, and re-layouts: 5.53 us -> 2.63 us
    unnamed x6 -> x0, waiting for transfers between devices: 100 us -> none
    dot_general x15 -> x0, matrix products: 58.1 us -> none  [the longest x3 36.5 us: moe_layer(): jnp.dot(hidden, down_w, preferred_element_type=jnp.float32)]
    pallas_call x0 -> x1, Pallas kernels: none -> 52.8 us  [body(): pl.pallas_call(functools.partial(window_kernel, sizes), out_shape=(jax.Sh...]
    all_gather x3 -> x0, blocking collectives: 40.2 us -> none  [moe_layer(): lax.all_gather(arrived.reshape(slots_all, width), 'expert', axis=0, tiled...]
    all_to_all x4 -> x0, blocking collectives: 14.9 us -> none  [the longest x3 11.2 us: moe_layer(): lax.all_to_all(answer, 'pair', split_axis=0, concat_axis=0, tiled=True)]
    ppermute x6 -> x0, starting transfers between devices: 10.7 us -> none  [shifted(): return lax.ppermute(block, axis, route)]
    all_to_all x2 -> x0, starting transfers between devices: 6.49 us -> none  [moe_layer(): lax.all_to_all(parcel, 'pair', split_axis=0, concat_axis=0, tiled=True)]
    ppermute x6 -> x0, waiting for transfers between devices: 6.48 us -> none  [shifted(): return lax.ppermute(block, axis, route)]
  transfers between devices with their start and end apart: 11 -> 0, of which waited for: 6 -> 0; matrix products, arithmetic and copies ran while one was open for 24% -> 0% of each run, Pallas kernels for 0% -> 0%
where the time goes in v2:
time: 56.5 us; the launch traced here: 56 us
  Pallas kernels  52.8 us (93%)
  local copies, waits for them, and re-layouts  2.63 us (5%)
  between operations  0.64 us (1%)
    pallas_call x1, Pallas kernels, body(): pl.pallas_call(functools.partial(window_kernel, sizes), out_shape=(jax.Sh...  52.8 us
    unnamed x2, local copies, waits for them, and re-layouts  2.63 us

profile of v2, /device:TPU:0, one launch (start us, length us, event | category | flops | bytes accessed | tf_op | source)
XLA Modules:
  0.0 56.0 jit_solution(3988046113124782275)
XLA Ops:
  0.6 52.8 %shard_map.95 = (bf16[1,2,3072]{2,1,0:T(2,128)(2,1)}, bf16[1,2,3072]{2,1,0:T(2,128)(2,1)}) custom-call(bf16[1,2,3072]{2,1,0:T(2,128)(2,1)} %act.1, bf16[1,2,3072]{2,1,0:T(2,128)(2,1)} %queue.1, s32[1,2,1,3]{3,2,1,0:T(1,128)} %bitcast.3, f32[1,3072]{1,0:T(1,128)} %gain.1, bf16[1,2,3072]{2,1,0:T(2,128)(2,1)} %bitcast.2, bf16[1,1,3072,2048]{3,2,1,0:T(8,128)(2,1)} %gate_hbm.1, ...), custom_call_target="tpu_custom_call" | custom-call | tf_op jit(solution)/shard_map/pallas_call | solution.py:541
  53.4 1.3 %copy.12 = bf16[1,2,3072]{2,1,0:T(2,128)(2,1)} copy(bf16[1,2,3072]{2,1,0:T(2,128)(2,1)} %get-tuple-element.4) | data formatting | bytes 24576
  54.7 1.3 %copy.13 = bf16[1,2,3072]{2,1,0:T(2,128)(2,1)} copy(bf16[1,2,3072]{2,1,0:T(2,128)(2,1)} %get-tuple-element.5) | data formatting | bytes 24576

commit v3 on v2

--- a/solution.py
+++ b/solution.py
@@ -20,8 +20,9 @@
 
 
 def window_kernel(
-    sizes, act, queue, picks, gain, table, gate_hbm, up_hbm, down_hbm, inflight, finished, *scratch
+    sizes, act, queue, picks, gain, table, gate_hbm, up_hbm, down_hbm, out, *scratch
 ):
+    inflight, finished = out.at[0:1], out.at[1:2]
     sections, chips, pairs, ticks, tok, width, hidden_w, fw, dw, levels = sizes
     fc, dc = hidden_w // fw, width // dw
     wide_row = width + 128
@@ -538,12 +539,9 @@
     sizes = (sections, chips, pairs, ticks, tok, width, hidden_w, fw, dw, levels)
     in_vmem = pl.BlockSpec(memory_space=pltpu.VMEM)
     anywhere = pl.BlockSpec(memory_space=pl.ANY)
-    return pl.pallas_call(
+    both = pl.pallas_call(
         functools.partial(window_kernel, sizes),
-        out_shape=(
-            jax.ShapeDtypeStruct(act.shape, BF16),
-            jax.ShapeDtypeStruct(act.shape, BF16),
-        ),
+        out_shape=jax.ShapeDtypeStruct((2, tok, width), BF16),
         in_specs=[
             in_vmem,
             in_vmem,
@@ -554,12 +552,13 @@
             anywhere,
             anywhere,
         ],
-        out_specs=(in_vmem, in_vmem),
+        out_specs=in_vmem,
         scratch_shapes=scratch,
         compiler_params=pltpu.CompilerParams(
             collective_id=0, has_side_effects=True, vmem_limit_bytes=60 * 1024 * 1024
         ),
     )(act, queue, jnp.transpose(picks, (0, 2, 3, 1)), gain, jnp.swapaxes(table, 1, 2), gate_w, up_w, down_w)
+    return both[0:1], both[1:2]
 
 
 def solution(mesh):

time: 56.5 us -> 55.1 us (0.975)
  local copies, waits for them, and re-layouts: 2.63 us -> 1.35 us
    unnamed x2 -> x0, local copies, waits for them, and re-layouts: 2.63 us -> none
    slice x0 -> x1, local copies, waits for them, and re-layouts: none -> 1.35 us  [body(): return (both[0:1], both[1:2])]
where the time goes in v3:
time: 55.1 us; the launch traced here: 54.7 us
  Pallas kernels  52.7 us (96%)
  local copies, waits for them, and re-layouts  1.35 us (2%)
  between operations  0.64 us (1%)
    pallas_call x1, Pallas kernels, body(): pl.pallas_call(functools.partial(window_kernel, sizes), out_shape=jax.Sha...  52.7 us
    slice x1, local copies, waits for them, and re-layouts, body(): return (both[0:1], both[1:2])  1.35 us

profile of v3, /device:TPU:0, one launch (start us, length us, event | category | flops | bytes accessed | tf_op | source)
XLA Modules:
  0.0 54.7 jit_solution(11617746792537140319)
XLA Ops:
  0.6 52.7 %shard_map.95 = bf16[2,2,3072]{2,1,0:T(2,128)(2,1)} custom-call(bf16[1,2,3072]{2,1,0:T(2,128)(2,1)} %act.1, bf16[1,2,3072]{2,1,0:T(2,128)(2,1)} %queue.1, s32[1,2,1,3]{3,2,1,0:T(1,128)} %bitcast.3, f32[1,3072]{1,0:T(1,128)} %gain.1, bf16[1,2,3072]{2,1,0:T(2,128)(2,1)} %bitcast.2, bf16[1,1,3072,2048]{3,2,1,0:T(8,128)(2,1)} %gate_hbm.1, ...), custom_call_target="tpu_custom_call" | custom-call | tf_op jit(solution)/shard_map/pallas_call | solution.py:542
  53.4 1.3 %fusion = (bf16[1,2,3072]{2,1,0:T(2,128)(2,1)}, bf16[1,2,3072]{2,1,0:T(2,128)(2,1)}) fusion(bf16[2,2,3072]{2,1,0:T(2,128)(2,1)} %shard_map.95), kind=kLoop, calls=%fused_computation | loop fusion | bytes 49152 | tf_op jit(solution)/shard_map/slice | solution.py:561
